TPU v7x, 32 devices: a whole 2x2x4 slice. The times are simulated.
32 devices in a mesh: gx: 4 (over z), gy: 2 (over core), ta: 4 (over y, x).
Axes of the slice: x: 2, y: 2, z: 4, core: 2. Of those that a mesh axis runs over, the one named last changes fastest.
Arguments:
- links: float32 [4, 2, 3, 3, 8, 4, 4, 128], P(None, None, None, None, 'gx', 'gy', 'ta'), may hold values from -1 to 1, as said below
Outputs:
- flowed: float32 [4, 2, 3, 3, 8, 4, 4, 128], P(None, None, None, None, 'gx', 'gy', 'ta')
- action_slices: float32 [4], P('ta')
Inputs may be any that keep to these rules, and one draw needn't show every extreme that they name: `links`: every link is a special unitary 3x3 matrix.
All inputs are finite; a program needn't handle non-finite values.
Results may differ from a plain program's by a relative error of at most 0.0003.
Values sent between devices are 32-bit elements; how exact they have to be, the bound alone decides.
A program may use at most 64 MiB of HBM per device.

v0:
```python
import jax
import jax.numpy as jnp
from jax import lax
from jax.sharding import PartitionSpec as P

flow_eps = 0.1
taylor_order = 6


def padded_2(shard, sides, width):
    for axis, dim in sides:
        devices, length = (lax.axis_size(axis), shard.shape[dim])
        up = [(i, (i + 1) % devices) for i in range(devices)]
        down = [(j, i) for i, j in up]
        last = lax.slice_in_dim(shard, length - width, length, axis=dim)
        initial = lax.slice_in_dim(shard, 0, width, axis=dim)
        before = lax.ppermute(last, axis, up)
        after = lax.ppermute(initial, axis, down)
        shard = jnp.concatenate([before, shard, after], axis=dim)
    return shard


def contract(first_part, second_part):
    return jnp.sum(first_part[:, :, None] * second_part[None, :, :], axis=1)


def matmul_pair(former, latter):
    return jnp.stack(
        [
            contract(former[0], latter[0]) - contract(former[1], latter[1]),
            contract(former[0], latter[1]) + contract(former[1], latter[0]),
        ]
    )


def adjoint(matrix):
    return jnp.stack([jnp.swapaxes(matrix[0], 0, 1), -jnp.swapaxes(matrix[1], 0, 1)])


def trace_real(former, latter):
    return jnp.sum(
        former[0] * jnp.swapaxes(latter[0], 0, 1) - former[1] * jnp.swapaxes(latter[1], 0, 1),
        axis=(0, 1),
    )


def unit_offset(dir_index, sign):
    return tuple((sign if k == dir_index else 0 for k in range(4)))


def add_offsets(first_off, second_off):
    return tuple((first_off[k] + second_off[k] for k in range(4)))


def shifted(component, offset):
    x_len = component.shape[-4] - 2
    y_len = component.shape[-3] - 2
    t_len = component.shape[-2] - 2
    view = component[
        ...,
        1 + offset[0] : 1 + offset[0] + x_len,
        1 + offset[1] : 1 + offset[1] + y_len,
        1 + offset[2] : 1 + offset[2] + t_len,
        :,
    ]
    if offset[3] != 0:
        view = jnp.roll(view, -offset[3], axis=-1)
    return view


def upper_staple(padded, mu_dir, nu_dir):
    here = (0, 0, 0, 0)
    first_pair = matmul_pair(
        shifted(padded[nu_dir], unit_offset(mu_dir, 1)),
        adjoint(shifted(padded[mu_dir], unit_offset(nu_dir, 1))),
    )
    return matmul_pair(first_pair, adjoint(shifted(padded[nu_dir], here)))


def lower_corner(padded, mu_dir, nu_dir):
    back = unit_offset(nu_dir, -1)
    corner = add_offsets(unit_offset(mu_dir, 1), back)
    first_pair = matmul_pair(
        adjoint(shifted(padded[nu_dir], corner)), adjoint(shifted(padded[mu_dir], back))
    )
    return matmul_pair(first_pair, shifted(padded[nu_dir], back))


def antihermitian(matrix):
    real_part = (matrix[0] - jnp.swapaxes(matrix[0], 0, 1)) / 2.0
    imag_part = (matrix[1] + jnp.swapaxes(matrix[1], 0, 1)) / 2.0
    trace_imag = jnp.trace(matrix[1], axis1=0, axis2=1) / 3.0
    eye = jnp.eye(3, dtype=jnp.float32).reshape((3, 3) + (1,) * (matrix.ndim - 3))
    return jnp.stack([real_part, imag_part - eye * trace_imag])


def flow_force(padded, lower_fn):
    centre = padded[..., 1:-1, 1:-1, 1:-1, :]
    forces = []
    action = jnp.zeros((centre.shape[6],), jnp.float32)
    for mu_dir in range(4):
        link_here = centre[mu_dir]
        staple_sum = jnp.zeros_like(link_here)
        for nu_dir in range(4):
            if nu_dir == mu_dir:
                continue
            upper = upper_staple(padded, mu_dir, nu_dir)
            action = action + jnp.sum(1.0 - trace_real(link_here, upper) / 3.0, axis=(0, 1, 3))
            staple_sum = staple_sum + upper + lower_fn(mu_dir, nu_dir)
        omega = matmul_pair(link_here, staple_sum)
        forces.append(-flow_eps * antihermitian(omega))
    return (jnp.stack(forces), action / 2.0)


def polynomial_exp(generator):
    eye = jnp.eye(3, dtype=jnp.float32).reshape((3, 3) + (1,) * (generator.ndim - 3))
    identity = jnp.stack(
        [jnp.broadcast_to(eye, generator.shape[1:]), jnp.zeros(generator.shape[1:], jnp.float32)]
    )
    result = identity
    for order in range(taylor_order, 0, -1):
        result = identity + matmul_pair(generator, result) / order
    return result


def advance(generator, links_now):

    def one_direction(gen_dir, link_dir):
        return matmul_pair(polynomial_exp(gen_dir), link_dir)

    return jax.vmap(one_direction)(generator, links_now)


def section_force(links_now):
    padded = padded_2(links_now, (("gx", 4), ("gy", 5), ("ta", 6)), 1)

    def lower_fn(mu_dir, nu_dir):
        return lower_corner(padded, mu_dir, nu_dir)

    return flow_force(padded, lower_fn)


def local(links):
    force_zero, action = section_force(links)
    section_one = advance(force_zero / 4.0, links)
    force_one, unused_one = section_force(section_one)
    section_two = advance(8.0 / 9.0 * force_one - 17.0 / 36.0 * force_zero, section_one)
    force_two, unused_two = section_force(section_two)
    flowed = advance(
        3.0 / 4.0 * force_two - 8.0 / 9.0 * force_one + 17.0 / 36.0 * force_zero, section_two
    )
    total = lax.psum(action, ("gx", "gy"))
    sites_slice = (
        6.0
        * links.shape[4]
        * lax.axis_size("gx")
        * links.shape[5]
        * lax.axis_size("gy")
        * links.shape[7]
    )
    return (flowed, total / sites_slice)


def solution(mesh):
    placed = (P(None, None, None, None, "gx", "gy", "ta", None),)
    return jax.shard_map(
        local,
        mesh=mesh,
        in_specs=placed,
        out_specs=(P(None, None, None, None, "gx", "gy", "ta", None), P("ta")),
        check_vma=False,
    )
```

profile of v0, /device:TPU:0, one launch (start us, length us, event | category | flops | bytes accessed | tf_op | source)
XLA Modules:
  0.0 176.6 jit_solution(15546038743013486022)
XLA Ops:
  0.6 1.0 fusion.394
  1.7 3.1 %collective-permute-start = (f32[4,2,3,3,1,2,1,128]{7,6,5,4,3,2,1,0:T(1,128)S(1)}, f32[4,2,3,3,1,2,1,128]{7,6,5,4,3,2,1,0:T(1,128)S(1)}, u32[]{:S(2)}, u32[]{:S(2)}) collective-permute-start(f32[4,2,3,3,1,2,1,128]{7,6,5,4,3,2,1,0:T(1,128)S(1)} %get-tuple-element.1159), channel_id=1, source_target_pairs={{0,8},{8,16},{16,24},{24,0},{1,9},{9,17},{17,25},{25,1},{2,10},{10... | collective-permute-start | bytes 221192 | tf_op jit(solution)/shard_map/ppermute | solution.py:17
  4.8 2.1 %collective-permute-start.1 = (f32[4,2,3,3,1,2,1,128]{7,6,5,4,3,2,1,0:T(1,128)S(1)}, f32[4,2,3,3,1,2,1,128]{7,6,5,4,3,2,1,0:T(1,128)S(1)}, u32[]{:S(2)}, u32[]{:S(2)}) collective-permute-start(f32[4,2,3,3,1,2,1,128]{7,6,5,4,3,2,1,0:T(1,128)S(1)} %get-tuple-element.1158), channel_id=1, source_target_pairs={{8,0},{16,8},{24,16},{0,24},{9,1},{17,9},{25,17},{1,25},{10,2},{18... | collective-permute-start | bytes 221192 | tf_op jit(solution)/shard_map/ppermute | solution.py:18
  6.9 2.4 %collective-permute-done = f32[4,2,3,3,1,2,1,128]{7,6,5,4,3,2,1,0:T(1,128)S(1)} collective-permute-done((f32[4,2,3,3,1,2,1,128]{7,6,5,4,3,2,1,0:T(1,128)S(1)}, f32[4,2,3,3,1,2,1,128]{7,6,5,4,3,2,1,0:T(1,128)S(1)}, u32[]{:S(2)}, u32[]{:S(2)}) %collective-permute-start) | collective-permute-done | bytes 73760 | tf_op jit(solution)/shard_map/ppermute | solution.py:17
  9.3 1.0 constant_dynamic-update-slice_fusion.1
  10.7 0.5 collective-permute-start.3
  11.2 0.9 collective-permute-done.2
  12.3 0.5 pad_maximum_fusion.3
  12.8 2.0 %collective-permute-start.4 = (f32[4,2,3,3,4,4,1,128]{7,6,5,4,3,2,1,0:T(1,128)S(1)}, f32[4,2,3,3,4,4,1,128]{7,6,5,4,3,2,1,0:T(1,128)S(1)}, u32[]{:S(2)}, u32[]{:S(2)}) collective-permute-start(f32[4,2,3,3,4,4,1,128]{7,6,5,4,3,2,1,0:T(1,128)S(1)} %pad_maximum_fusion.3), channel_id=1, source_target_pairs={{0,1},{1,2},{2,3},{3,0},{4,5},{5,6},{6,7},{7,4},{8,9},{9,10},{10,1... | collective-permute-start | bytes 1769480 | tf_op jit(solution)/shard_map/ppermute | solution.py:17
  14.8 1.0 collective-permute-start.5
  16.3 13.6 %collective-permute-done.4 = f32[4,2,3,3,4,4,1,128]{7,6,5,4,3,2,1,0:T(1,128)S(1)} collective-permute-done((f32[4,2,3,3,4,4,1,128]{7,6,5,4,3,2,1,0:T(1,128)S(1)}, f32[4,2,3,3,4,4,1,128]{7,6,5,4,3,2,1,0:T(1,128)S(1)}, u32[]{:S(2)}, u32[]{:S(2)}) %collective-permute-start.4) | collective-permute-done | bytes 589856 | tf_op jit(solution)/shard_map/ppermute | solution.py:17
  30.0 12.5 %collective-permute-done.5 = f32[4,2,3,3,4,4,1,128]{7,6,5,4,3,2,1,0:T(1,128)S(1)} collective-permute-done((f32[4,2,3,3,4,4,1,128]{7,6,5,4,3,2,1,0:T(1,128)S(1)}, f32[4,2,3,3,4,4,1,128]{7,6,5,4,3,2,1,0:T(1,128)S(1)}, u32[]{:S(2)}, u32[]{:S(2)}) %collective-permute-start.5) | collective-permute-done | bytes 589856 | tf_op jit(solution)/shard_map/ppermute | solution.py:18
  42.4 2.2 %pad_maximum_fusion = f32[4,2,3,3,4,4,3,128]{7,6,5,4,3,2,1,0:T(4,128)S(1)} fusion(f32[4,2,3,3,4,4,1,128]{7,6,5,4,3,2,1,0:T(1,128)S(1)} %collective-permute-done.5, f32[4,2,3,3,4,1,1,128]{7,6,5,4,3,2,1,0:T(1,128)S(1)} %collective-permute-done.3, f32[4,2,3,3,4,2,1,128]{7,6,5,4,3,2,1,0:T(1,128)S(1)} %constant_dynamic-update-slice_fusion, ...), kind=kLoop, calls=%fused_computation | loop fusion | flops 1769472 | bytes 3538944 | tf_op jit(solution)/shard_map/concatenate | solution.py:19
  44.6 0.8 slice_bitcast_fusion
  45.7 0.4 fusion.361
  60.1 0.7 subtract_reduce_fusion.2
  60.8 0.6 subtract_reduce_fusion.5
  61.4 0.6 subtract_reduce_fusion.8
  64.6 0.4 collective-permute-start.6
  65.1 3.4 %collective-permute-start.7 = (f32[4,2,3,3,1,2,1,128]{7,0,5,4,3,2,6,1:T(4,128)S(1)}, f32[4,2,3,3,1,2,1,128]{7,0,5,4,3,2,6,1:T(4,128)S(1)}, u32[]{:S(2)}, u32[]{:S(2)}) collective-permute-start(f32[4,2,3,3,1,2,1,128]{7,0,5,4,3,2,6,1:T(4,128)S(1)} %get-tuple-element.1133), channel_id=1, source_target_pairs={{8,0},{16,8},{24,16},{0,24},{9,1},{17,9},{25,17},{1,25},{10,2},{18... | collective-permute-start | bytes 221192 | tf_op jit(solution)/shard_map/ppermute | solution.py:18
  68.5 0.6 subtract_reduce_fusion.10
  69.1 1.8 %collective-permute-done.6 = f32[4,2,3,3,1,2,1,128]{7,0,5,4,3,2,6,1:T(4,128)S(1)} collective-permute-done((f32[4,2,3,3,1,2,1,128]{7,0,5,4,3,2,6,1:T(4,128)S(1)}, f32[4,2,3,3,1,2,1,128]{7,0,5,4,3,2,6,1:T(4,128)S(1)}, u32[]{:S(2)}, u32[]{:S(2)}) %collective-permute-start.6) | collective-permute-done | bytes 73760 | tf_op jit(solution)/shard_map/ppermute | solution.py:17
  71.1 0.5 collective-permute-start.9
  71.6 0.6 subtract_reduce_fusion.11
  72.2 0.7 subtract_reduce_fusion.9
  73.0 1.5 collective-permute-start.10
  74.6 1.4 collective-permute-start.11
  76.0 0.7 subtract_reduce_fusion.7
  76.7 0.6 subtract_reduce_fusion.6
  77.4 12.8 %collective-permute-done.10 = f32[4,2,3,3,4,4,1,128]{7,0,5,4,3,2,6,1:T(4,128)S(1)} collective-permute-done((f32[4,2,3,3,4,4,1,128]{7,0,5,4,3,2,6,1:T(4,128)S(1)}, f32[4,2,3,3,4,4,1,128]{7,0,5,4,3,2,6,1:T(4,128)S(1)}, u32[]{:S(2)}, u32[]{:S(2)}) %collective-permute-start.10) | collective-permute-done | bytes 589856 | tf_op jit(solution)/shard_map/ppermute | solution.py:17
  90.2 10.9 %collective-permute-done.11 = f32[4,2,3,3,4,4,1,128]{7,0,5,4,3,2,6,1:T(4,128)S(1)} collective-permute-done((f32[4,2,3,3,4,4,1,128]{7,0,5,4,3,2,6,1:T(4,128)S(1)}, f32[4,2,3,3,4,4,1,128]{7,0,5,4,3,2,6,1:T(4,128)S(1)}, u32[]{:S(2)}, u32[]{:S(2)}) %collective-permute-start.11) | collective-permute-done | bytes 589856 | tf_op jit(solution)/shard_map/ppermute | solution.py:18
  101.1 0.5 pad_maximum_fusion.1
  101.5 1.3 fusion.359
  113.2 0.4 multiply_reduce_fusion.440
  115.1 0.4 fusion.77
  118.9 3.8 %collective-permute-start.13 = (f32[4,2,3,3,1,2,1,128]{7,0,5,4,3,2,6,1:T(4,128)S(1)}, f32[4,2,3,3,1,2,1,128]{7,0,5,4,3,2,6,1:T(4,128)S(1)}, u32[]{:S(2)}, u32[]{:S(2)}) collective-permute-start(f32[4,2,3,3,1,2,1,128]{7,0,5,4,3,2,6,1:T(4,128)S(1)} %get-tuple-element.1107), channel_id=1, source_target_pairs={{8,0},{16,8},{24,16},{0,24},{9,1},{17,9},{25,17},{1,25},{10,2},{18... | collective-permute-start | bytes 221192 | tf_op jit(solution)/shard_map/ppermute | solution.py:18
  122.7 0.6 subtract_reduce_fusion.4
  123.3 2.3 %collective-permute-done.12 = f32[4,2,3,3,1,2,1,128]{7,0,5,4,3,2,6,1:T(4,128)S(1)} collective-permute-done((f32[4,2,3,3,1,2,1,128]{7,0,5,4,3,2,6,1:T(4,128)S(1)}, f32[4,2,3,3,1,2,1,128]{7,0,5,4,3,2,6,1:T(4,128)S(1)}, u32[]{:S(2)}, u32[]{:S(2)}) %collective-permute-start.12) | collective-permute-done | bytes 73760 | tf_op jit(solution)/shard_map/ppermute | solution.py:17
  125.8 0.5 collective-permute-start.15
  126.3 0.6 subtract_reduce_fusion.3
  126.9 0.6 subtract_reduce_fusion.1
  127.7 1.7 collective-permute-start.16
  129.4 1.2 collective-permute-start.17
  130.7 0.7 subtract_reduce_fusion
  138.9 17.1 %psum.7 = f32[1]{0:T(128)} all-reduce(f32[1]{0:T(128)} %bitcast.1282), channel_id=1, replica_groups=mesh['gx'=4,'gy'=2,'ta'=4] {'gx','gy'}, use_global_device_ids=true, to_apply=%region_744.745 | all-reduce | flops 1 | bytes 8 | tf_op jit(solution)/shard_map/psum | solution.py:152
  156.9 0.5 pad_maximum_fusion.2
  157.4 1.3 fusion.358
  174.4 0.8 copy.1082
  (700 shorter events, 45.9 us)
Async XLA Ops:
  0.6 15.4 %copy-start = (f32[4,2,3,3,2,2,1,128]{7,6,5,4,3,2,1,0:T(1,128)S(1)}, f32[4,2,3,3,2,2,1,128]{7,6,5,4,3,2,1,0:T(1,128)}, u32[]{:S(2)}) copy-start(f32[4,2,3,3,2,2,1,128]{7,6,5,4,3,2,1,0:T(1,128)} %param.1) | copy-start | bytes 442372
  1.7 7.6 %collective-permute-start = (f32[4,2,3,3,1,2,1,128]{7,6,5,4,3,2,1,0:T(1,128)S(1)}, f32[4,2,3,3,1,2,1,128]{7,6,5,4,3,2,1,0:T(1,128)S(1)}, u32[]{:S(2)}, u32[]{:S(2)}) collective-permute-start(f32[4,2,3,3,1,2,1,128]{7,6,5,4,3,2,1,0:T(1,128)S(1)} %get-tuple-element.1159), channel_id=1, source_target_pairs={{0,8},{8,16},{16,24},{24,0},{1,9},{9,17},{17,25},{25,1},{2,10},{10... | collective-permute-start | bytes 221192 | tf_op jit(solution)/shard_map/ppermute | solution.py:17
  4.8 5.6 %collective-permute-start.1 = (f32[4,2,3,3,1,2,1,128]{7,6,5,4,3,2,1,0:T(1,128)S(1)}, f32[4,2,3,3,1,2,1,128]{7,6,5,4,3,2,1,0:T(1,128)S(1)}, u32[]{:S(2)}, u32[]{:S(2)}) collective-permute-start(f32[4,2,3,3,1,2,1,128]{7,6,5,4,3,2,1,0:T(1,128)S(1)} %get-tuple-element.1158), channel_id=1, source_target_pairs={{8,0},{16,8},{24,16},{0,24},{9,1},{17,9},{25,17},{1,25},{10,2},{18... | collective-permute-start | bytes 221192 | tf_op jit(solution)/shard_map/ppermute | solution.py:18
  10.6 1.4 collective-permute-start.2
  10.7 1.6 collective-permute-start.3
  12.8 17.2 %collective-permute-start.4 = (f32[4,2,3,3,4,4,1,128]{7,6,5,4,3,2,1,0:T(1,128)S(1)}, f32[4,2,3,3,4,4,1,128]{7,6,5,4,3,2,1,0:T(1,128)S(1)}, u32[]{:S(2)}, u32[]{:S(2)}) collective-permute-start(f32[4,2,3,3,4,4,1,128]{7,6,5,4,3,2,1,0:T(1,128)S(1)} %pad_maximum_fusion.3), channel_id=1, source_target_pairs={{0,1},{1,2},{2,3},{3,0},{4,5},{5,6},{6,7},{7,4},{8,9},{9,10},{10,1... | collective-permute-start | bytes 1769480 | tf_op jit(solution)/shard_map/ppermute | solution.py:17
  14.8 27.6 %collective-permute-start.5 = (f32[4,2,3,3,4,4,1,128]{7,6,5,4,3,2,1,0:T(1,128)S(1)}, f32[4,2,3,3,4,4,1,128]{7,6,5,4,3,2,1,0:T(1,128)S(1)}, u32[]{:S(2)}, u32[]{:S(2)}) collective-permute-start(f32[4,2,3,3,4,4,1,128]{7,6,5,4,3,2,1,0:T(1,128)S(1)} %pad_maximum_fusion.3), channel_id=1, source_target_pairs={{1,0},{2,1},{3,2},{0,3},{5,4},{6,5},{7,6},{4,7},{9,8},{10,9},{11,1... | collective-permute-start | bytes 1769480 | tf_op jit(solution)/shard_map/ppermute | solution.py:18
  64.6 6.3 %collective-permute-start.6 = (f32[4,2,3,3,1,2,1,128]{7,0,5,4,3,2,6,1:T(4,128)S(1)}, f32[4,2,3,3,1,2,1,128]{7,0,5,4,3,2,6,1:T(4,128)S(1)}, u32[]{:S(2)}, u32[]{:S(2)}) collective-permute-start(f32[4,2,3,3,1,2,1,128]{7,0,5,4,3,2,6,1:T(4,128)S(1)} %get-tuple-element.1132), channel_id=1, source_target_pairs={{0,8},{8,16},{16,24},{24,0},{1,9},{9,17},{17,25},{25,1},{2,10},{10... | collective-permute-start | bytes 221192 | tf_op jit(solution)/shard_map/ppermute | solution.py:17
  65.1 5.8 %collective-permute-start.7 = (f32[4,2,3,3,1,2,1,128]{7,0,5,4,3,2,6,1:T(4,128)S(1)}, f32[4,2,3,3,1,2,1,128]{7,0,5,4,3,2,6,1:T(4,128)S(1)}, u32[]{:S(2)}, u32[]{:S(2)}) collective-permute-start(f32[4,2,3,3,1,2,1,128]{7,0,5,4,3,2,6,1:T(4,128)S(1)} %get-tuple-element.1133), channel_id=1, source_target_pairs={{8,0},{16,8},{24,16},{0,24},{9,1},{17,9},{25,17},{1,25},{10,2},{18... | collective-permute-start | bytes 221192 | tf_op jit(solution)/shard_map/ppermute | solution.py:18
  71.0 1.9 %collective-permute-start.8 = (f32[4,2,3,3,4,1,1,128]{7,0,5,4,3,2,6,1:T(4,128)S(1)}, f32[4,2,3,3,4,1,1,128]{7,0,5,4,3,2,6,1:T(4,128)S(1)}, u32[]{:S(2)}, u32[]{:S(2)}) collective-permute-start(f32[4,2,3,3,4,1,1,128]{7,0,5,4,3,2,6,1:T(4,128)S(1)} %get-tuple-element.1077), channel_id=1, source_target_pairs={{0,4},{4,0},{1,5},{5,1},{2,6},{6,2},{3,7},{7,3},{8,12},{12,8},{9,1... | collective-permute-start | bytes 442376 | tf_op jit(solution)/shard_map/ppermute | solution.py:17
  71.1 1.8 %collective-permute-start.9 = (f32[4,2,3,3,4,1,1,128]{7,0,5,4,3,2,6,1:T(4,128)S(1)}, f32[4,2,3,3,4,1,1,128]{7,0,5,4,3,2,6,1:T(4,128)S(1)}, u32[]{:S(2)}, u32[]{:S(2)}) collective-permute-start(f32[4,2,3,3,4,1,1,128]{7,0,5,4,3,2,6,1:T(4,128)S(1)} %get-tuple-element.1078), channel_id=1, source_target_pairs={{4,0},{0,4},{5,1},{1,5},{6,2},{2,6},{7,3},{3,7},{12,8},{8,12},{13,... | collective-permute-start | bytes 442376 | tf_op jit(solution)/shard_map/ppermute | solution.py:18
  73.0 17.2 %collective-permute-start.10 = (f32[4,2,3,3,4,4,1,128]{7,0,5,4,3,2,6,1:T(4,128)S(1)}, f32[4,2,3,3,4,4,1,128]{7,0,5,4,3,2,6,1:T(4,128)S(1)}, u32[]{:S(2)}, u32[]{:S(2)}) collective-permute-start(f32[4,2,3,3,4,4,1,128]{7,0,5,4,3,2,6,1:T(4,128)S(1)} %pad_maximum_fusion.4), channel_id=1, source_target_pairs={{0,1},{1,2},{2,3},{3,0},{4,5},{5,6},{6,7},{7,4},{8,9},{9,10},{10,1... | collective-permute-start | bytes 1769480 | tf_op jit(solution)/shard_map/ppermute | solution.py:17
  74.6 26.5 %collective-permute-start.11 = (f32[4,2,3,3,4,4,1,128]{7,0,5,4,3,2,6,1:T(4,128)S(1)}, f32[4,2,3,3,4,4,1,128]{7,0,5,4,3,2,6,1:T(4,128)S(1)}, u32[]{:S(2)}, u32[]{:S(2)}) collective-permute-start(f32[4,2,3,3,4,4,1,128]{7,0,5,4,3,2,6,1:T(4,128)S(1)} %pad_maximum_fusion.4), channel_id=1, source_target_pairs={{1,0},{2,1},{3,2},{0,3},{5,4},{6,5},{7,6},{4,7},{9,8},{10,9},{11,1... | collective-permute-start | bytes 1769480 | tf_op jit(solution)/shard_map/ppermute | solution.py:18
  118.8 6.8 %collective-permute-start.12 = (f32[4,2,3,3,1,2,1,128]{7,0,5,4,3,2,6,1:T(4,128)S(1)}, f32[4,2,3,3,1,2,1,128]{7,0,5,4,3,2,6,1:T(4,128)S(1)}, u32[]{:S(2)}, u32[]{:S(2)}) collective-permute-start(f32[4,2,3,3,1,2,1,128]{7,0,5,4,3,2,6,1:T(4,128)S(1)} %get-tuple-element.1106), channel_id=1, source_target_pairs={{0,8},{8,16},{16,24},{24,0},{1,9},{9,17},{17,25},{25,1},{2,10},{10... | collective-permute-start | bytes 221192 | tf_op jit(solution)/shard_map/ppermute | solution.py:17
  118.9 6.7 %collective-permute-start.13 = (f32[4,2,3,3,1,2,1,128]{7,0,5,4,3,2,6,1:T(4,128)S(1)}, f32[4,2,3,3,1,2,1,128]{7,0,5,4,3,2,6,1:T(4,128)S(1)}, u32[]{:S(2)}, u32[]{:S(2)}) collective-permute-start(f32[4,2,3,3,1,2,1,128]{7,0,5,4,3,2,6,1:T(4,128)S(1)} %get-tuple-element.1107), channel_id=1, source_target_pairs={{8,0},{16,8},{24,16},{0,24},{9,1},{17,9},{25,17},{1,25},{10,2},{18... | collective-permute-start | bytes 221192 | tf_op jit(solution)/shard_map/ppermute | solution.py:18
  125.8 1.8 %collective-permute-start.14 = (f32[4,2,3,3,4,1,1,128]{7,0,5,4,3,2,6,1:T(4,128)S(1)}, f32[4,2,3,3,4,1,1,128]{7,0,5,4,3,2,6,1:T(4,128)S(1)}, u32[]{:S(2)}, u32[]{:S(2)}) collective-permute-start(f32[4,2,3,3,4,1,1,128]{7,0,5,4,3,2,6,1:T(4,128)S(1)} %get-tuple-element.1075), channel_id=1, source_target_pairs={{0,4},{4,0},{1,5},{5,1},{2,6},{6,2},{3,7},{7,3},{8,12},{12,8},{9,1... | collective-permute-start | bytes 442376 | tf_op jit(solution)/shard_map/ppermute | solution.py:17
  125.8 1.7 collective-permute-start.15
  127.7 29.1 %collective-permute-start.16 = (f32[4,2,3,3,4,4,1,128]{7,0,5,4,3,2,6,1:T(4,128)S(1)}, f32[4,2,3,3,4,4,1,128]{7,0,5,4,3,2,6,1:T(4,128)S(1)}, u32[]{:S(2)}, u32[]{:S(2)}) collective-permute-start(f32[4,2,3,3,4,4,1,128]{7,0,5,4,3,2,6,1:T(4,128)S(1)} %pad_maximum_fusion.5), channel_id=1, source_target_pairs={{0,1},{1,2},{2,3},{3,0},{4,5},{5,6},{6,7},{7,4},{8,9},{9,10},{10,1... | collective-permute-start | bytes 1769480 | tf_op jit(solution)/shard_map/ppermute | solution.py:17
  129.4 27.5 %collective-permute-start.17 = (f32[4,2,3,3,4,4,1,128]{7,0,5,4,3,2,6,1:T(4,128)S(1)}, f32[4,2,3,3,4,4,1,128]{7,0,5,4,3,2,6,1:T(4,128)S(1)}, u32[]{:S(2)}, u32[]{:S(2)}) collective-permute-start(f32[4,2,3,3,4,4,1,128]{7,0,5,4,3,2,6,1:T(4,128)S(1)} %pad_maximum_fusion.5), channel_id=1, source_target_pairs={{1,0},{2,1},{3,2},{0,3},{5,4},{6,5},{7,6},{4,7},{9,8},{10,9},{11,1... | collective-permute-start | bytes 1769480 | tf_op jit(solution)/shard_map/ppermute | solution.py:18
where the time goes:
time: 180 us; the launch traced here: 177 us
  waiting for transfers between devices  57.4 us (32%)
  other arithmetic  52.5 us (29%)
  starting transfers between devices  23.6 us (13%)
  blocking collectives  17.1 us (10%)
  between operations  14.5 us (8%)
  local copies, waits for them, and re-layouts  11.3 us (6%)
    ppermute x9, waiting for transfers between devices, padded_2(): before = lax.ppermute(last, axis, up)  33.8 us
    reduce_sum x135, other arithmetic, contract(): return jnp.sum(first_part[:, :, None] * second_part[None, :, :], axis=1)  23.8 us
    ppermute x9, waiting for transfers between devices, padded_2(): after = lax.ppermute(initial, axis, down)  23.6 us
    psum x1, blocking collectives, local(): total = lax.psum(action, ('gx', 'gy'))  17.1 us
    ppermute x9, starting transfers between devices, padded_2(): after = lax.ppermute(initial, axis, down)  14.5 us
    ppermute x9, starting transfers between devices, padded_2(): before = lax.ppermute(last, axis, up)  9.14 us
    reduce_sum x12, other arithmetic, flow_force(): jnp.sum(1.0 - trace_real(link_here, upper) / 3.0, axis=(0, 1, 3))  7.55 us
    concatenate x8, other arithmetic, padded_2(): shard = jnp.concatenate([before, shard, after], axis=dim)  4.09 us
  transfers between devices with their start and end apart: 18, of which 10 were waited for; matrix products, arithmetic and copies ran while one was open for 4% of the time, Pallas kernels for 0%

commit v1 on v0

v1 whole, which is shorter than its diff:
```python
import functools

import jax
import jax.numpy as jnp
from jax import lax
from jax.experimental import pallas as pl
from jax.experimental.pallas import tpu as pltpu
from jax.sharding import PartitionSpec as P

MESH = pl.DeviceIdType.MESH
AXES = ("gx", "gy", "ta")
flow_eps = 0.1
FRESH = (1.0 / 4.0, 8.0 / 9.0, 3.0 / 4.0)
KEPT = (0.0, -17.0 / 9.0, -1.0)


def mul(a, b):
    def dot(x, y):
        return sum(x[:, k][:, None] * y[k][None] for k in range(3))

    return dot(a[0], b[0]) - dot(a[1], b[1]), dot(a[0], b[1]) + dot(a[1], b[0])


def mul_right_adjoint(a, b):
    def dot(x, y):
        return sum(x[:, k][:, None] * y[:, k][None] for k in range(3))

    return dot(a[0], b[0]) + dot(a[1], b[1]), dot(a[1], b[0]) - dot(a[0], b[1])


def mul_left_adjoint(a, b):
    def dot(x, y):
        return sum(x[k][:, None] * y[k][None] for k in range(3))

    return dot(a[0], b[0]) + dot(a[1], b[1]), dot(a[0], b[1]) - dot(a[1], b[0])


def add(a, b):
    return b if a is None else (a[0] + b[0], a[1] + b[1])


def projected(m):
    r, i = m
    third = (i[0, 0] + i[1, 1] + i[2, 2]) / 3.0
    parts = [i[j, j] - third for j in range(3)]
    for j, k in ((0, 1), (0, 2), (1, 2)):
        parts += [(r[j, k] - r[k, j]) / 2.0, (i[j, k] + i[k, j]) / 2.0]
    return jnp.stack(parts)


def exponential(g):
    h = [g[0], g[1], g[2]]
    u, v, w = (g[3], g[4]), (g[5], g[6]), (g[7], g[8])
    nu, nv, nw = (z[0] * z[0] + z[1] * z[1] for z in (u, v, w))
    uw = (u[0] * w[0] - u[1] * w[1], u[0] * w[1] + u[1] * w[0])
    diag = [h[0] * h[0] + nu + nv, h[1] * h[1] + nu + nw, h[2] * h[2] + nv + nw]
    p = -0.5 * (diag[0] + diag[1] + diag[2])
    det = (
        h[0] * (h[1] * h[2] - nw)
        - h[1] * nv
        - h[2] * nu
        + 2.0 * (uw[1] * v[0] - uw[0] * v[1])
    )
    s01, s02, s12 = h[0] + h[1], h[0] + h[2], h[1] + h[2]
    square = {
        (0, 1): (
            -s01 * u[1] - (v[0] * w[0] + v[1] * w[1]),
            s01 * u[0] - (v[1] * w[0] - v[0] * w[1]),
        ),
        (0, 2): (-s02 * v[1] + uw[0], s02 * v[0] + uw[1]),
        (1, 2): (
            -s12 * w[1] - (u[0] * v[0] + u[1] * v[1]),
            s12 * w[0] - (u[0] * v[1] - u[1] * v[0]),
        ),
    }
    line = {(0, 1): u, (0, 2): v, (1, 2): w}
    ai4, br4 = det * (-1.0 / 120.0), 0.25 + p * (1.0 / 120.0)
    ai3, br3, bi3, cr3 = (
        det * (-1.0 / 60.0),
        1.0 / 3.0 + p * (1.0 / 60.0),
        ai4 * (1.0 / 3.0),
        br4 * (1.0 / 3.0),
    )
    ai2, br2, bi2, cr2, ci2 = (
        det * cr3 * -0.5,
        0.5 + 0.5 * p * cr3,
        0.5 * ai3,
        0.5 * br3,
        0.5 * bi3,
    )
    ar, ai = 1.0 + det * ci2, -det * cr2
    br, bi, cr, ci = 1.0 + p * cr2, ai2 + p * ci2, br2, bi2
    re = [[None] * 3 for _ in range(3)]
    im = [[None] * 3 for _ in range(3)]
    for j in range(3):
        re[j][j] = ar - bi * h[j] - cr * diag[j]
        im[j][j] = ai + br * h[j] - ci * diag[j]
    for j, k in line:
        x, s = line[j, k], square[j, k]
        even_r, odd_r = br * x[0], bi * x[1]
        even_i, odd_i = br * x[1], bi * x[0]
        cs = (cr * s[0], ci * s[1], cr * s[1], ci * s[0])
        re[j][k] = (even_r - odd_r) + (cs[0] - cs[1])
        im[j][k] = (even_i + odd_i) + (cs[2] + cs[3])
        re[k][j] = -(even_r + odd_r) + (cs[0] + cs[1])
        im[k][j] = (even_i - odd_i) + (cs[3] - cs[2])
    return (
        jnp.stack([jnp.stack(row) for row in re]),
        jnp.stack([jnp.stack(row) for row in im]),
    )


def runs(pairs):
    out = []
    for to, frm in pairs:
        if out and to == out[-1][0] + out[-1][2] and frm == out[-1][1] + out[-1][2]:
            out[-1][2] += 1
        else:
            out.append([to, frm, 1])
    return out


def neighbour_rows(block, offset):
    lx, ly, lt = block
    found = {}
    for row in range(lx * ly * lt):
        site = (row // (ly * lt), row // lt % ly, row % lt)
        moved = [site[k] + offset[k] for k in range(3)]
        step = tuple(moved[k] // block[k] for k in range(3))
        at = [moved[k] % block[k] for k in range(3)]
        frm = (at[0] * ly + at[1]) * lt + at[2]
        found.setdefault(step, []).append((row, frm))
    return found


def unit(k, sign):
    return tuple(sign if j == k else 0 for j in range(3))


CORNERS = [(m, n) for m in range(3) for n in range(3) if m != n]


def plan_of(block):
    remote, local = [], []
    for k in range(3):
        for kind, sign in (("minus", -1), ("plus", 1)):
            spans = [(0, 4)]
            if kind == "plus":
                spans = [(a, b) for a, b in ((0, k), (k + 1, 4)) if b > a]
            for step, pairs in neighbour_rows(block, unit(k, sign)).items():
                for to, frm, n in runs(pairs):
                    for a, b in spans:
                        item = (kind, k, a, b - a, to, frm, n)
                        if any(step):
                            remote.append(item + (step,))
                        else:
                            local.append(item)
    inner = []
    for c, (m, n) in enumerate(CORNERS):
        ahead, behind = unit(m, 1), unit(n, -1)
        rows_ahead = dict(neighbour_rows(block, ahead).get((0, 0, 0), []))
        rows_behind = dict(neighbour_rows(block, behind).get((0, 0, 0), []))
        offset = tuple(ahead[j] + behind[j] for j in range(3))
        from_minus, from_plus = [], []
        for step, pairs in neighbour_rows(block, offset).items():
            outer = []
            for to, frm in pairs:
                if to in rows_ahead:
                    from_minus.append((to, rows_ahead[to]))
                elif to in rows_behind:
                    from_plus.append((to, rows_behind[to]))
                else:
                    outer.append((to, frm))
            for to, frm, count in runs(outer):
                remote.append(("corner", c, n, 1, to, frm, count, step))
        for to, frm, count in runs(sorted(from_minus)):
            inner.append((c, "minus", n, n, to, frm, count))
        for to, frm, count in runs(sorted(from_plus)):
            inner.append((c, "plus", m, n, to, frm, count))
    return remote, local, inner


def kernel(
    block,
    sizes,
    plan,
    partners,
    w_ref,
    out_ref,
    act_ref,
    cur_ref,
    plus_ref,
    minus_ref,
    corner_ref,
    gen_ref,
    part_ref,
    slot_ref,
    send_sem,
    recv_sem,
    act_send,
    act_recv,
):
    remote, local, inner = plan
    rows = block[0] * block[1] * block[2]
    lanes = w_ref.shape[-1]
    here = [lax.axis_index(axis) for axis in AXES]

    def device(step):
        return tuple(lax.rem(here[k] + step[k] + sizes[k], sizes[k]) for k in range(3))

    steps = sorted({item[-1] for item in remote})
    greeted = steps + partners
    barrier = pltpu.get_barrier_semaphore()
    for step in greeted:
        pl.semaphore_signal(barrier, inc=1, device_id=device(step), device_id_type=MESH)
    pl.semaphore_wait(barrier, len(greeted))

    side = {"plus": plus_ref, "minus": minus_ref}
    action_copies = []

    for stage in range(3):
        field = w_ref if stage == 0 else cur_ref.at[stage - 1]
        copies = []
        for j, (kind, index, first, dirs, to, frm, count, step) in enumerate(remote):
            if kind == "corner":
                dst = corner_ref.at[stage, pl.ds(index, 1), :, :, :, pl.ds(to, count), :]
            else:
                dst = side[kind].at[
                    stage, index, pl.ds(first, dirs), :, :, :, pl.ds(to, count), :
                ]
            copy = pltpu.make_async_remote_copy(
                src_ref=field.at[pl.ds(first, dirs), :, :, :, pl.ds(frm, count), :],
                dst_ref=dst,
                send_sem=send_sem.at[stage, j],
                recv_sem=recv_sem.at[stage, j],
                device_id=device(tuple(-s for s in step)),
                device_id_type=MESH,
            )
            copy.start()
            copies.append(copy)
        for kind, index, first, dirs, to, frm, count in local:
            side[kind][stage, index, first : first + dirs, :, :, :, to : to + count, :] = field[
                first : first + dirs, :, :, :, frm : frm + count, :
            ]
        for copy in copies:
            copy.wait()
        for c, kind, index, n, to, frm, count in inner:
            corner_ref[stage, c, :, :, :, to : to + count, :] = side[kind][
                stage, index, n, :, :, :, frm : frm + count, :
            ]

        def centre(mu):
            return field[mu, 0], field[mu, 1]

        def roll(pair, shift):
            return tuple(pltpu.roll(x, shift % lanes, axis=3) for x in pair)

        def ahead(nu, mu):
            if mu == 3:
                return roll(centre(nu), -1)
            return plus_ref[stage, mu, nu, 0], plus_ref[stage, mu, nu, 1]

        def behind(mu, nu):
            return minus_ref[stage, nu, mu, 0], minus_ref[stage, nu, mu, 1]

        def corner(mu, nu):
            if mu == 3:
                return roll(behind(nu, nu), -1)
            c = CORNERS.index((mu, nu))
            return corner_ref[stage, c, 0], corner_ref[stage, c, 1]

        upper, lower = [None] * 4, [None] * 4
        action = None
        for mu in range(4):
            for nu in range(mu + 1, 4):
                one = mul(centre(mu), ahead(nu, mu))
                two = mul(centre(nu), ahead(mu, nu))
                plaq = mul_right_adjoint(one, two)
                if stage == 0:
                    trace = plaq[0][0, 0] + plaq[0][1, 1] + plaq[0][2, 2]
                    term = 1.0 - trace / 3.0
                    action = term if action is None else action + term
                flux = projected(plaq)
                upper[mu] = flux if upper[mu] is None else upper[mu] + flux
                upper[nu] = -flux if upper[nu] is None else upper[nu] - flux
                if nu == 3:
                    low = roll(mul_left_adjoint(one, centre(3)), 1)
                    lower[mu] = add(lower[mu], low)
        for mu in range(4):
            for nu in range(3):
                if nu != mu:
                    one = mul(behind(mu, nu), corner(mu, nu))
                    lower[mu] = add(lower[mu], mul_left_adjoint(one, behind(nu, nu)))
            omega = projected(mul(centre(mu), lower[mu])) + upper[mu]
            gen = (-flow_eps * FRESH[stage]) * omega
            if stage:
                gen = gen + KEPT[stage] * gen_ref[mu]
            if stage < 2:
                gen_ref[mu] = gen
            moved = mul(exponential(gen), centre(mu))
            if stage < 2:
                cur_ref[stage, mu, 0] = moved[0]
                cur_ref[stage, mu, 1] = moved[1]
            else:
                out_ref[mu, 0] = moved[0]
                out_ref[mu, 1] = moved[1]
        if stage == 0:
            lt = block[2]
            for t in range(lt):
                line = sum(action[r : r + 1] for r in range(t, rows, lt))
                part_ref[t : t + 1, :] = line
            mine = here[0] * sizes[1] + here[1]
            for j, step in enumerate(partners):
                copy = pltpu.make_async_remote_copy(
                    src_ref=part_ref,
                    dst_ref=slot_ref.at[mine],
                    send_sem=act_send.at[j],
                    recv_sem=act_recv.at[j],
                    device_id=device(step),
                    device_id_type=MESH,
                )
                copy.start()
                action_copies.append(copy)
            slot_ref[mine] = part_ref[...]
    for copy in action_copies:
        copy.wait()
    total = sum(slot_ref[j] for j in range(sizes[0] * sizes[1]))
    scale = 1.0 / (6.0 * sizes[0] * sizes[1] * block[0] * block[1] * lanes)
    total = jnp.sum(total, axis=1, keepdims=True) * scale
    act_ref[...] = jnp.broadcast_to(total, act_ref.shape)


def solution(mesh):
    sizes = tuple(mesh.shape[axis] for axis in AXES)

    def local(links):
        block = links.shape[4:7]
        lanes = links.shape[7]
        rows = block[0] * block[1] * block[2]
        plan = plan_of(block)
        partners = [
            (i, j, 0) for i in range(sizes[0]) for j in range(sizes[1]) if i or j
        ]
        count = len(plan[0])
        matrix = (2, 3, 3, rows, lanes)
        f32 = jnp.float32
        vmem = pl.BlockSpec(memory_space=pltpu.VMEM)
        flowed, action = pl.pallas_call(
            functools.partial(kernel, block, sizes, plan, partners),
            out_shape=(
                jax.ShapeDtypeStruct((4,) + matrix, f32),
                jax.ShapeDtypeStruct((block[2], lanes), f32),
            ),
            in_specs=[vmem],
            out_specs=(vmem, vmem),
            scratch_shapes=[
                pltpu.VMEM((2, 4) + matrix, f32),
                pltpu.VMEM((3, 3, 4) + matrix, f32),
                pltpu.VMEM((3, 3, 4) + matrix, f32),
                pltpu.VMEM((3, len(CORNERS)) + matrix, f32),
                pltpu.VMEM((4, 9, rows, lanes), f32),
                pltpu.VMEM((block[2], lanes), f32),
                pltpu.VMEM((sizes[0] * sizes[1], block[2], lanes), f32),
                pltpu.SemaphoreType.DMA((3, count)),
                pltpu.SemaphoreType.DMA((3, count)),
                pltpu.SemaphoreType.DMA((len(partners),)),
                pltpu.SemaphoreType.DMA((len(partners),)),
            ],
            compiler_params=pltpu.CompilerParams(
                collective_id=0, has_side_effects=True, vmem_limit_bytes=48 * 2**20
            ),
        )(links.reshape((4,) + matrix))
        return flowed.reshape(links.shape), action[:, 0]

    spec = P(None, None, None, None, "gx", "gy", "ta", None)
    return jax.shard_map(
        local, mesh=mesh, in_specs=(spec,), out_specs=(spec, P("ta")), check_vma=False
    )
```

time: 180 us -> 42.9 us (0.24); the launches traced: 177 us -> 42.7 us
  waiting for transfers between devices: 57.4 us -> 0 us
  other arithmetic: 52.5 us -> 0 us
  Pallas kernels: 0 us -> 39.3 us
  starting transfers between devices: 23.6 us -> 0 us
  blocking collectives: 17.1 us -> 0 us
  between operations: 14.5 us -> 1.81 us
  local copies, waits for them, and re-layouts: 11.3 us -> 1.57 us
    ppermute x18 -> x0, waiting for transfers between devices: 57.4 us -> none  [the longest x9 33.8 us: padded_2(): before = lax.ppermute(last, axis, up)]
    pallas_call x0 -> x1, Pallas kernels: none -> 39.3 us  [local(): pl.pallas_call(functools.partial(kernel, block, sizes, plan, partners), o...]
    reduce_sum x154 -> x0, other arithmetic: 32 us -> none  [the longest x135 23.8 us: contract(): return jnp.sum(first_part[:, :, None] * second_part[None, :, :], axis=1)]
    ppermute x18 -> x0, starting transfers between devices: 23.6 us -> none  [the longest x9 14.5 us: padded_2(): after = lax.ppermute(initial, axis, down)]
    psum x1 -> x0, blocking collectives: 17.1 us -> none  [local(): total = lax.psum(action, ('gx', 'gy'))]
    slice x32 -> x0, local copies, waits for them, and re-layouts: 7.79 us -> none  [the longest x20 3.49 us: shifted(): view = jnp.roll(view, -offset[3], axis=-1)]
    concatenate x15 -> x0, other arithmetic: 5.1 us -> none  [the longest x8 4.09 us: padded_2(): shard = jnp.concatenate([before, shard, after], axis=dim)]
    another operation x201 -> x0, other arithmetic: 4.13 us -> none  [the longest x174 2.65 us: matmul_pair(): jnp.stack([contract(former[0], latter[0]) - contract(former[1], latter[1]...]
  transfers between devices with their start and end apart: 18 -> 0, of which waited for: 10 -> 0; matrix products, arithmetic and copies ran while one was open for 4% -> 0% of each run, Pallas kernels for 0% -> 0%
where the time goes in v1:
time: 42.9 us; the launch traced here: 42.7 us
  Pallas kernels  39.3 us (92%)
  between operations  1.81 us (4%)
  local copies, waits for them, and re-layouts  1.57 us (4%)
    pallas_call x1, Pallas kernels, local(): pl.pallas_call(functools.partial(kernel, block, sizes, plan, partners), o...  39.3 us
    unnamed x3, local copies, waits for them, and re-layouts  1.57 us

profile of v1, /device:TPU:0, one launch (start us, length us, event | category | flops | bytes accessed | tf_op | source)
XLA Modules:
  0.0 42.7 jit_solution(3116269870789616244)
XLA Ops:
  0.6 0.0 copy-start
  0.6 0.9 %copy-done = f32[4,2,3,3,2,2,1,128]{7,6,5,4,3,2,1,0:T(1,128)S(1)} copy-done((f32[4,2,3,3,2,2,1,128]{7,6,5,4,3,2,1,0:T(1,128)S(1)}, f32[4,2,3,3,2,2,1,128]{7,6,5,4,3,2,1,0:T(1,128)}, u32[]{:S(2)}) %copy-start) | copy-done | bytes 147480
  1.5 39.3 %shard_map.30 = (f32[4,2,3,3,4,128]{5,4,3,2,1,0:T(4,128)S(1)}, f32[1,128]{1,0:T(1,128)S(1)}) custom-call(f32[4,2,3,3,4,128]{5,4,3,2,1,0:T(4,128)S(1)} %bitcast.6), custom_call_target="tpu_custom_call" | custom-call | tf_op jit(solution)/shard_map/pallas_call | solution.py:348
  40.8 0.7 %copy.6 = f32[4,2,3,3,2,2,1,128]{7,6,5,4,3,2,1,0:T(1,128)} copy(f32[4,2,3,3,2,2,1,128]{7,6,5,4,3,2,1,0:T(1,128)S(1)} %bitcast.7) | data formatting | bytes 294912
Async XLA Ops:
  0.6 0.9 %copy-start = (f32[4,2,3,3,2,2,1,128]{7,6,5,4,3,2,1,0:T(1,128)S(1)}, f32[4,2,3,3,2,2,1,128]{7,6,5,4,3,2,1,0:T(1,128)}, u32[]{:S(2)}) copy-start(f32[4,2,3,3,2,2,1,128]{7,6,5,4,3,2,1,0:T(1,128)} %param.1) | copy-start | bytes 442372

commit v2 on v1

--- a/solution.py
+++ b/solution.py
@@ -42,15 +42,15 @@
 def projected(m):
     r, i = m
     third = (i[0, 0] + i[1, 1] + i[2, 2]) / 3.0
-    parts = [i[j, j] - third for j in range(3)]
+    parts = [i[j, j] - third for j in range(2)]
     for j, k in ((0, 1), (0, 2), (1, 2)):
         parts += [(r[j, k] - r[k, j]) / 2.0, (i[j, k] + i[k, j]) / 2.0]
     return jnp.stack(parts)
 
 
 def exponential(g):
-    h = [g[0], g[1], g[2]]
-    u, v, w = (g[3], g[4]), (g[5], g[6]), (g[7], g[8])
+    h = [g[0], g[1], -(g[0] + g[1])]
+    u, v, w = (g[2], g[3]), (g[4], g[5]), (g[6], g[7])
     nu, nv, nw = (z[0] * z[0] + z[1] * z[1] for z in (u, v, w))
     uw = (u[0] * w[0] - u[1] * w[1], u[0] * w[1] + u[1] * w[0])
     diag = [h[0] * h[0] + nu + nv, h[1] * h[1] + nu + nw, h[2] * h[2] + nv + nw]
@@ -137,46 +137,56 @@
     return tuple(sign if j == k else 0 for j in range(3))
 
 
-CORNERS = [(m, n) for m in range(3) for n in range(3) if m != n]
+PAIRS = [(0, 1), (0, 2), (1, 2)]
+
+
+def place(m, n):
+    return PAIRS.index((min(m, n), max(m, n))), int(m > n)
 
 
 def plan_of(block):
     remote, local = [], []
     for k in range(3):
-        for kind, sign in (("minus", -1), ("plus", 1)):
+        for half, sign in ((0, -1), (1, 1)):
             spans = [(0, 4)]
-            if kind == "plus":
+            if half:
                 spans = [(a, b) for a, b in ((0, k), (k + 1, 4)) if b > a]
             for step, pairs in neighbour_rows(block, unit(k, sign)).items():
                 for to, frm, n in runs(pairs):
                     for a, b in spans:
-                        item = (kind, k, a, b - a, to, frm, n)
+                        item = (int(k == 2), "face", k, half, a, b - a, to, frm, n)
                         if any(step):
                             remote.append(item + (step,))
                         else:
                             local.append(item)
     inner = []
-    for c, (m, n) in enumerate(CORNERS):
-        ahead, behind = unit(m, 1), unit(n, -1)
-        rows_ahead = dict(neighbour_rows(block, ahead).get((0, 0, 0), []))
-        rows_behind = dict(neighbour_rows(block, behind).get((0, 0, 0), []))
-        offset = tuple(ahead[j] + behind[j] for j in range(3))
-        from_minus, from_plus = [], []
-        for step, pairs in neighbour_rows(block, offset).items():
-            outer = []
-            for to, frm in pairs:
-                if to in rows_ahead:
-                    from_minus.append((to, rows_ahead[to]))
-                elif to in rows_behind:
-                    from_plus.append((to, rows_behind[to]))
-                else:
-                    outer.append((to, frm))
-            for to, frm, count in runs(outer):
-                remote.append(("corner", c, n, 1, to, frm, count, step))
-        for to, frm, count in runs(sorted(from_minus)):
-            inner.append((c, "minus", n, n, to, frm, count))
-        for to, frm, count in runs(sorted(from_plus)):
-            inner.append((c, "plus", m, n, to, frm, count))
+    for m in range(3):
+        for n in range(3):
+            if m == n:
+                continue
+            c, half = place(m, n)
+            ahead, behind = unit(m, 1), unit(n, -1)
+            rows_ahead = dict(neighbour_rows(block, ahead).get((0, 0, 0), []))
+            rows_behind = dict(neighbour_rows(block, behind).get((0, 0, 0), []))
+            offset = tuple(ahead[j] + behind[j] for j in range(3))
+            group = int(2 in (m, n))
+            from_minus, from_plus = [], []
+            for step, pairs in neighbour_rows(block, offset).items():
+                outer = []
+                for to, frm in pairs:
+                    if to in rows_ahead:
+                        from_minus.append((to, rows_ahead[to]))
+                    elif to in rows_behind:
+                        from_plus.append((to, rows_behind[to]))
+                    else:
+                        outer.append((to, frm))
+                for to, frm, count in runs(outer):
+                    remote.append((group, "corner", c, half, n, 1, to, frm, count, step))
+            for to, frm, count in runs(sorted(from_minus)):
+                inner.append((group, c, half, n, 0, n, to, frm, count))
+            for to, frm, count in runs(sorted(from_plus)):
+                inner.append((group, c, half, m, 1, n, to, frm, count))
+    remote.sort(key=lambda item: -item[0])
     return remote, local, inner
 
 
@@ -189,10 +199,11 @@
     out_ref,
     act_ref,
     cur_ref,
-    plus_ref,
-    minus_ref,
+    face_ref,
     corner_ref,
     gen_ref,
+    gen_face_ref,
+    gen_corner_ref,
     part_ref,
     slot_ref,
     send_sem,
@@ -215,21 +226,28 @@
         pl.semaphore_signal(barrier, inc=1, device_id=device(step), device_id_type=MESH)
     pl.semaphore_wait(barrier, len(greeted))
 
-    side = {"plus": plus_ref, "minus": minus_ref}
-    action_copies = []
+    started, action_copies = [], []
 
     for stage in range(3):
         field = w_ref if stage == 0 else cur_ref.at[stage - 1]
         copies = []
-        for j, (kind, index, first, dirs, to, frm, count, step) in enumerate(remote):
-            if kind == "corner":
-                dst = corner_ref.at[stage, pl.ds(index, 1), :, :, :, pl.ds(to, count), :]
+        for j, item in enumerate(remote):
+            group, kind, index, half, first, dirs, to, frm, count, step = item
+            span, put, take = pl.ds(first, dirs), pl.ds(half * rows + to, count), pl.ds(frm, count)
+            if stage == 0:
+                src = w_ref.at[span, :, pl.ds(0, 2), :, take, :]
+                if kind == "corner":
+                    dst = corner_ref.at[pl.ds(index, 1), :, pl.ds(0, 2), :, put, :]
+                else:
+                    dst = face_ref.at[index, span, :, pl.ds(0, 2), :, put, :]
             else:
-                dst = side[kind].at[
-                    stage, index, pl.ds(first, dirs), :, :, :, pl.ds(to, count), :
-                ]
+                src = gen_ref.at[stage - 1, span, :, take, :]
+                if kind == "corner":
+                    dst = gen_corner_ref.at[stage - 1, pl.ds(index, 1), :, put, :]
+                else:
+                    dst = gen_face_ref.at[stage - 1, index, span, :, put, :]
             copy = pltpu.make_async_remote_copy(
-                src_ref=field.at[pl.ds(first, dirs), :, :, :, pl.ds(frm, count), :],
+                src_ref=src,
                 dst_ref=dst,
                 send_sem=send_sem.at[stage, j],
                 recv_sem=recv_sem.at[stage, j],
@@ -237,17 +255,51 @@
                 device_id_type=MESH,
             )
             copy.start()
-            copies.append(copy)
-        for kind, index, first, dirs, to, frm, count in local:
-            side[kind][stage, index, first : first + dirs, :, :, :, to : to + count, :] = field[
-                first : first + dirs, :, :, :, frm : frm + count, :
-            ]
-        for copy in copies:
-            copy.wait()
-        for c, kind, index, n, to, frm, count in inner:
-            corner_ref[stage, c, :, :, :, to : to + count, :] = side[kind][
-                stage, index, n, :, :, :, frm : frm + count, :
-            ]
+            copies.append((group, copy))
+            started.append(copy)
+        for group, kind, index, half, first, dirs, to, frm, count in local:
+            low = half * rows + to
+            if stage == 0:
+                face_ref[index, first : first + dirs, :, 0:2, :, low : low + count, :] = w_ref[
+                    first : first + dirs, :, 0:2, :, frm : frm + count, :
+                ]
+            else:
+                gen_face_ref[stage - 1, index, first : first + dirs, :, low : low + count, :] = (
+                    gen_ref[stage - 1, first : first + dirs, :, frm : frm + count, :]
+                )
+
+        def renew(ref, generator):
+            if stage == 0:
+                r, i = ref[0, 0:2], ref[1, 0:2]
+                for j in range(3):
+                    k, l = (j + 1) % 3, (j + 2) % 3
+                    ref[0, 2, j] = (r[0, k] * r[1, l] - i[0, k] * i[1, l]) - (
+                        r[0, l] * r[1, k] - i[0, l] * i[1, k]
+                    )
+                    ref[1, 2, j] = (r[0, l] * i[1, k] + i[0, l] * r[1, k]) - (
+                        r[0, k] * i[1, l] + i[0, k] * r[1, l]
+                    )
+            else:
+                new = mul(exponential(generator[...]), (ref[0], ref[1]))
+                ref[0] = new[0]
+                ref[1] = new[1]
+
+        def arrive(wanted):
+            for group, copy in copies:
+                if group == wanted:
+                    copy.wait_recv()
+            for k in (0, 1) if wanted == 0 else (2,):
+                for mu in range(4):
+                    renew(face_ref.at[k, mu], gen_face_ref.at[max(stage - 1, 0), k, mu])
+            for c, pair in enumerate(PAIRS):
+                if int(2 in pair) == wanted:
+                    renew(corner_ref.at[c], gen_corner_ref.at[max(stage - 1, 0), c])
+            for group, c, half, k, side, n, to, frm, count in inner:
+                if group == wanted:
+                    put, take = half * rows + to, side * rows + frm
+                    corner_ref[c, :, :, :, put : put + count, :] = face_ref[
+                        k, n, :, :, :, take : take + count, :
+                    ]
 
         def centre(mu):
             return field[mu, 0], field[mu, 1]
@@ -255,48 +307,55 @@
         def roll(pair, shift):
             return tuple(pltpu.roll(x, shift % lanes, axis=3) for x in pair)
 
+        def part(ref, index, half):
+            low = half * rows
+            return tuple(ref[index + (c, slice(None), slice(None), slice(low, low + rows))] for c in range(2))
+
         def ahead(nu, mu):
-            if mu == 3:
-                return roll(centre(nu), -1)
-            return plus_ref[stage, mu, nu, 0], plus_ref[stage, mu, nu, 1]
+            return roll(centre(nu), -1) if mu == 3 else part(face_ref, (mu, nu), 1)
 
         def behind(mu, nu):
-            return minus_ref[stage, nu, mu, 0], minus_ref[stage, nu, mu, 1]
+            return part(face_ref, (nu, mu), 0)
 
         def corner(mu, nu):
             if mu == 3:
                 return roll(behind(nu, nu), -1)
-            c = CORNERS.index((mu, nu))
-            return corner_ref[stage, c, 0], corner_ref[stage, c, 1]
+            c, half = place(mu, nu)
+            return part(corner_ref, (c,), half)
 
         upper, lower = [None] * 4, [None] * 4
         action = None
+        for wanted in (0, 1):
+            arrive(wanted)
+            for mu in range(4):
+                for nu in range(mu + 1, 4):
+                    if int(2 in (mu, nu)) != wanted:
+                        continue
+                    one = mul(centre(mu), ahead(nu, mu))
+                    two = mul(centre(nu), ahead(mu, nu))
+                    plaq = mul_right_adjoint(one, two)
+                    if stage == 0:
+                        trace = plaq[0][0, 0] + plaq[0][1, 1] + plaq[0][2, 2]
+                        term = 1.0 - trace / 3.0
+                        action = term if action is None else action + term
+                    flux = projected(plaq)
+                    upper[mu] = flux if upper[mu] is None else upper[mu] + flux
+                    upper[nu] = -flux if upper[nu] is None else upper[nu] - flux
+                    if nu == 3:
+                        low = roll(mul_left_adjoint(one, centre(3)), 1)
+                        lower[mu] = add(lower[mu], low)
+            for mu in range(4):
+                for nu in range(3):
+                    if nu != mu and int(2 in (mu, nu)) == wanted:
+                        one = mul(behind(mu, nu), corner(mu, nu))
+                        lower[mu] = add(lower[mu], mul_left_adjoint(one, behind(nu, nu)))
         for mu in range(4):
-            for nu in range(mu + 1, 4):
-                one = mul(centre(mu), ahead(nu, mu))
-                two = mul(centre(nu), ahead(mu, nu))
-                plaq = mul_right_adjoint(one, two)
-                if stage == 0:
-                    trace = plaq[0][0, 0] + plaq[0][1, 1] + plaq[0][2, 2]
-                    term = 1.0 - trace / 3.0
-                    action = term if action is None else action + term
-                flux = projected(plaq)
-                upper[mu] = flux if upper[mu] is None else upper[mu] + flux
-                upper[nu] = -flux if upper[nu] is None else upper[nu] - flux
-                if nu == 3:
-                    low = roll(mul_left_adjoint(one, centre(3)), 1)
-                    lower[mu] = add(lower[mu], low)
-        for mu in range(4):
-            for nu in range(3):
-                if nu != mu:
-                    one = mul(behind(mu, nu), corner(mu, nu))
-                    lower[mu] = add(lower[mu], mul_left_adjoint(one, behind(nu, nu)))
             omega = projected(mul(centre(mu), lower[mu])) + upper[mu]
             gen = (-flow_eps * FRESH[stage]) * omega
             if stage:
-                gen = gen + KEPT[stage] * gen_ref[mu]
+                gen = gen + KEPT[stage] * gen_ref[stage - 1, mu]
             if stage < 2:
-                gen_ref[mu] = gen
+                gen_ref[stage, mu] = gen
             moved = mul(exponential(gen), centre(mu))
             if stage < 2:
                 cur_ref[stage, mu, 0] = moved[0]
@@ -322,6 +381,8 @@
                 copy.start()
                 action_copies.append(copy)
             slot_ref[mine] = part_ref[...]
+    for copy in started:
+        copy.wait_send()
     for copy in action_copies:
         copy.wait()
     total = sum(slot_ref[j] for j in range(sizes[0] * sizes[1]))
@@ -343,6 +404,7 @@
         ]
         count = len(plan[0])
         matrix = (2, 3, 3, rows, lanes)
+        both = (2, 3, 3, 2 * rows, lanes)
         f32 = jnp.float32
         vmem = pl.BlockSpec(memory_space=pltpu.VMEM)
         flowed, action = pl.pallas_call(
@@ -355,10 +417,11 @@
             out_specs=(vmem, vmem),
             scratch_shapes=[
                 pltpu.VMEM((2, 4) + matrix, f32),
-                pltpu.VMEM((3, 3, 4) + matrix, f32),
-                pltpu.VMEM((3, 3, 4) + matrix, f32),
-                pltpu.VMEM((3, len(CORNERS)) + matrix, f32),
-                pltpu.VMEM((4, 9, rows, lanes), f32),
+                pltpu.VMEM((3, 4) + both, f32),
+                pltpu.VMEM((len(PAIRS),) + both, f32),
+                pltpu.VMEM((2, 4, 8, rows, lanes), f32),
+                pltpu.VMEM((2, 3, 4, 8, 2 * rows, lanes), f32),
+                pltpu.VMEM((2, len(PAIRS), 8, 2 * rows, lanes), f32),
                 pltpu.VMEM((block[2], lanes), f32),
                 pltpu.VMEM((sizes[0] * sizes[1], block[2], lanes), f32),
                 pltpu.SemaphoreType.DMA((3, count)),

time: 42.9 us -> 32.6 us (0.76)
  Pallas kernels: 39.3 us -> 29 us
    pallas_call x1, Pallas kernels: 39.3 us -> 29 us  [local(): pl.pallas_call(functools.partial(kernel, block, sizes, plan, partners), o...]
where the time goes in v2:
time: 32.6 us; the launch traced here: 32.4 us
  Pallas kernels  29 us (89%)
  between operations  1.81 us (6%)
  local copies, waits for them, and re-layouts  1.57 us (5%)
    pallas_call x1, Pallas kernels, local(): pl.pallas_call(functools.partial(kernel, block, sizes, plan, partners), o...  29 us
    unnamed x3, local copies, waits for them, and re-layouts  1.57 us

profile of v2, /device:TPU:0, one launch (start us, length us, event | category | flops | bytes accessed | tf_op | source)
XLA Modules:
  0.0 32.4 jit_solution(4772062209706764982)
XLA Ops:
  0.6 0.0 copy-start
  0.6 0.9 %copy-done = f32[4,2,3,3,2,2,1,128]{7,6,5,4,3,2,1,0:T(1,128)S(1)} copy-done((f32[4,2,3,3,2,2,1,128]{7,6,5,4,3,2,1,0:T(1,128)S(1)}, f32[4,2,3,3,2,2,1,128]{7,6,5,4,3,2,1,0:T(1,128)}, u32[]{:S(2)}) %copy-start) | copy-done | bytes 147480
  1.5 29.0 %shard_map.30 = (f32[4,2,3,3,4,128]{5,4,3,2,1,0:T(4,128)S(1)}, f32[1,128]{1,0:T(1,128)S(1)}) custom-call(f32[4,2,3,3,4,128]{5,4,3,2,1,0:T(4,128)S(1)} %bitcast.6), custom_call_target="tpu_custom_call" | custom-call | tf_op jit(solution)/shard_map/pallas_call | solution.py:410
  30.6 0.7 %copy.6 = f32[4,2,3,3,2,2,1,128]{7,6,5,4,3,2,1,0:T(1,128)} copy(f32[4,2,3,3,2,2,1,128]{7,6,5,4,3,2,1,0:T(1,128)S(1)} %bitcast.7) | data formatting | bytes 294912
Async XLA Ops:
  0.6 0.9 %copy-start = (f32[4,2,3,3,2,2,1,128]{7,6,5,4,3,2,1,0:T(1,128)S(1)}, f32[4,2,3,3,2,2,1,128]{7,6,5,4,3,2,1,0:T(1,128)}, u32[]{:S(2)}) copy-start(f32[4,2,3,3,2,2,1,128]{7,6,5,4,3,2,1,0:T(1,128)} %param.1) | copy-start | bytes 442372

commit v3 on v2

--- a/solution.py
+++ b/solution.py
@@ -169,7 +169,7 @@
             rows_ahead = dict(neighbour_rows(block, ahead).get((0, 0, 0), []))
             rows_behind = dict(neighbour_rows(block, behind).get((0, 0, 0), []))
             offset = tuple(ahead[j] + behind[j] for j in range(3))
-            group = int(2 in (m, n))
+            group = 2 * int(2 in (m, n))
             from_minus, from_plus = [], []
             for step, pairs in neighbour_rows(block, offset).items():
                 outer = []
@@ -186,7 +186,7 @@
                 inner.append((group, c, half, n, 0, n, to, frm, count))
             for to, frm, count in runs(sorted(from_plus)):
                 inner.append((group, c, half, m, 1, n, to, frm, count))
-    remote.sort(key=lambda item: -item[0])
+    remote.sort(key=lambda item: (item[1] == "face", -item[0]))
     return remote, local, inner
 
 
@@ -195,9 +195,10 @@
     sizes,
     plan,
     partners,
-    w_ref,
+    w_hbm,
     out_ref,
     act_ref,
+    w_ref,
     cur_ref,
     face_ref,
     corner_ref,
@@ -210,10 +211,13 @@
     recv_sem,
     act_send,
     act_recv,
+    load_sem,
 ):
     remote, local, inner = plan
     rows = block[0] * block[1] * block[2]
-    lanes = w_ref.shape[-1]
+    lanes = w_hbm.shape[-1]
+    load = pltpu.make_async_copy(w_hbm, w_ref, load_sem)
+    load.start()
     here = [lax.axis_index(axis) for axis in AXES]
 
     def device(step):
@@ -225,6 +229,7 @@
     for step in greeted:
         pl.semaphore_signal(barrier, inc=1, device_id=device(step), device_id_type=MESH)
     pl.semaphore_wait(barrier, len(greeted))
+    load.wait()
 
     started, action_copies = [], []
 
@@ -257,6 +262,31 @@
             copy.start()
             copies.append((group, copy))
             started.append(copy)
+        if stage:
+            before = w_ref if stage == 1 else cur_ref.at[stage - 2]
+            for mu in range(4):
+                own = (before[mu, 0], before[mu, 1])
+                moved = mul(exponential(gen_ref[stage - 1, mu]), own)
+                cur_ref[stage - 1, mu, 0] = moved[0]
+                cur_ref[stage - 1, mu, 1] = moved[1]
+        if stage == 1:
+            lt = block[2]
+            for t in range(lt):
+                line = sum(action[r : r + 1] for r in range(t, rows, lt))
+                part_ref[t : t + 1, :] = line
+            mine = here[0] * sizes[1] + here[1]
+            for j, step in enumerate(partners):
+                copy = pltpu.make_async_remote_copy(
+                    src_ref=part_ref,
+                    dst_ref=slot_ref.at[mine],
+                    send_sem=act_send.at[j],
+                    recv_sem=act_recv.at[j],
+                    device_id=device(step),
+                    device_id_type=MESH,
+                )
+                copy.start()
+                action_copies.append(copy)
+            slot_ref[mine] = part_ref[...]
         for group, kind, index, half, first, dirs, to, frm, count in local:
             low = half * rows + to
             if stage == 0:
@@ -288,11 +318,11 @@
             for group, copy in copies:
                 if group == wanted:
                     copy.wait_recv()
-            for k in (0, 1) if wanted == 0 else (2,):
+            for k in ((0, 1), (2,), ())[wanted]:
                 for mu in range(4):
                     renew(face_ref.at[k, mu], gen_face_ref.at[max(stage - 1, 0), k, mu])
             for c, pair in enumerate(PAIRS):
-                if int(2 in pair) == wanted:
+                if 2 * int(2 in pair) == wanted:
                     renew(corner_ref.at[c], gen_corner_ref.at[max(stage - 1, 0), c])
             for group, c, half, k, side, n, to, frm, count in inner:
                 if group == wanted:
@@ -324,8 +354,9 @@
             return part(corner_ref, (c,), half)
 
         upper, lower = [None] * 4, [None] * 4
-        action = None
-        for wanted in (0, 1):
+        if stage == 0:
+            action = None
+        for wanted in (0, 1, 2):
             arrive(wanted)
             for mu in range(4):
                 for nu in range(mu + 1, 4):
@@ -346,41 +377,21 @@
                         lower[mu] = add(lower[mu], low)
             for mu in range(4):
                 for nu in range(3):
-                    if nu != mu and int(2 in (mu, nu)) == wanted:
+                    late = int(2 in (mu, nu)) * (1 if mu == 3 else 2)
+                    if nu != mu and late == wanted:
                         one = mul(behind(mu, nu), corner(mu, nu))
                         lower[mu] = add(lower[mu], mul_left_adjoint(one, behind(nu, nu)))
-        for mu in range(4):
-            omega = projected(mul(centre(mu), lower[mu])) + upper[mu]
-            gen = (-flow_eps * FRESH[stage]) * omega
-            if stage:
-                gen = gen + KEPT[stage] * gen_ref[stage - 1, mu]
-            if stage < 2:
-                gen_ref[stage, mu] = gen
-            moved = mul(exponential(gen), centre(mu))
-            if stage < 2:
-                cur_ref[stage, mu, 0] = moved[0]
-                cur_ref[stage, mu, 1] = moved[1]
-            else:
-                out_ref[mu, 0] = moved[0]
-                out_ref[mu, 1] = moved[1]
-        if stage == 0:
-            lt = block[2]
-            for t in range(lt):
-                line = sum(action[r : r + 1] for r in range(t, rows, lt))
-                part_ref[t : t + 1, :] = line
-            mine = here[0] * sizes[1] + here[1]
-            for j, step in enumerate(partners):
-                copy = pltpu.make_async_remote_copy(
-                    src_ref=part_ref,
-                    dst_ref=slot_ref.at[mine],
-                    send_sem=act_send.at[j],
-                    recv_sem=act_recv.at[j],
-                    device_id=device(step),
-                    device_id_type=MESH,
-                )
-                copy.start()
-                action_copies.append(copy)
-            slot_ref[mine] = part_ref[...]
+            for mu in ((), (3,), (0, 1, 2))[wanted]:
+                omega = projected(mul(centre(mu), lower[mu])) + upper[mu]
+                gen = (-flow_eps * FRESH[stage]) * omega
+                if stage:
+                    gen = gen + KEPT[stage] * gen_ref[stage - 1, mu]
+                if stage < 2:
+                    gen_ref[stage, mu] = gen
+                else:
+                    moved = mul(exponential(gen), centre(mu))
+                    out_ref[mu, 0] = moved[0]
+                    out_ref[mu, 1] = moved[1]
     for copy in started:
         copy.wait_send()
     for copy in action_copies:
@@ -413,9 +424,10 @@
                 jax.ShapeDtypeStruct((4,) + matrix, f32),
                 jax.ShapeDtypeStruct((block[2], lanes), f32),
             ),
-            in_specs=[vmem],
+            in_specs=[pl.BlockSpec(memory_space=pltpu.HBM)],
             out_specs=(vmem, vmem),
             scratch_shapes=[
+                pltpu.VMEM((4,) + matrix, f32),
                 pltpu.VMEM((2, 4) + matrix, f32),
                 pltpu.VMEM((3, 4) + both, f32),
                 pltpu.VMEM((len(PAIRS),) + both, f32),
@@ -428,6 +440,7 @@
                 pltpu.SemaphoreType.DMA((3, count)),
                 pltpu.SemaphoreType.DMA((len(partners),)),
                 pltpu.SemaphoreType.DMA((len(partners),)),
+                pltpu.SemaphoreType.DMA,
             ],
             compiler_params=pltpu.CompilerParams(
                 collective_id=0, has_side_effects=True, vmem_limit_bytes=48 * 2**20

time: 32.6 us -> 31.6 us (0.969)
  Pallas kernels: 29 us -> 28.1 us
    pallas_call x1, Pallas kernels: 29 us -> 28.1 us  [local(): pl.pallas_call(functools.partial(kernel, block, sizes, plan, partners), o...]
where the time goes in v3:
time: 31.6 us; the launch traced here: 31.5 us
  Pallas kernels  28.1 us (89%)
  between operations  1.81 us (6%)
  local copies, waits for them, and re-layouts  1.57 us (5%)
    pallas_call x1, Pallas kernels, local(): pl.pallas_call(functools.partial(kernel, block, sizes, plan, partners), o...  28.1 us
    unnamed x3, local copies, waits for them, and re-layouts  1.57 us

profile of v3, /device:TPU:0, one launch (start us, length us, event | category | flops | bytes accessed | tf_op | source)
XLA Modules:
  0.0 31.5 jit_solution(14204240929217580476)
XLA Ops:
  0.6 0.0 copy-start
  0.6 0.9 %copy-done = f32[4,2,3,3,2,2,1,128]{7,6,5,4,3,2,1,0:T(1,128)S(1)} copy-done((f32[4,2,3,3,2,2,1,128]{7,6,5,4,3,2,1,0:T(1,128)S(1)}, f32[4,2,3,3,2,2,1,128]{7,6,5,4,3,2,1,0:T(1,128)}, u32[]{:S(2)}) %copy-start) | copy-done | bytes 147480
  1.5 28.1 %shard_map.30 = (f32[4,2,3,3,4,128]{5,4,3,2,1,0:T(4,128)S(1)}, f32[1,128]{1,0:T(1,128)S(1)}) custom-call(f32[4,2,3,3,4,128]{5,4,3,2,1,0:T(4,128)S(1)} %bitcast.6), custom_call_target="tpu_custom_call" | custom-call | tf_op jit(solution)/shard_map/pallas_call | solution.py:421
  29.6 0.7 %copy.6 = f32[4,2,3,3,2,2,1,128]{7,6,5,4,3,2,1,0:T(1,128)} copy(f32[4,2,3,3,2,2,1,128]{7,6,5,4,3,2,1,0:T(1,128)S(1)} %bitcast.7) | data formatting | bytes 294912
Async XLA Ops:
  0.6 0.9 %copy-start = (f32[4,2,3,3,2,2,1,128]{7,6,5,4,3,2,1,0:T(1,128)S(1)}, f32[4,2,3,3,2,2,1,128]{7,6,5,4,3,2,1,0:T(1,128)}, u32[]{:S(2)}) copy-start(f32[4,2,3,3,2,2,1,128]{7,6,5,4,3,2,1,0:T(1,128)} %param.1) | copy-start | bytes 442372
